TPU v7x, 32 devices: a whole 2x2x4 slice. The times are simulated.
32 devices in a mesh: groups: 1, expert: 16 (over z, y, x), tensor: 2 (over core).
Axes of the slice: x: 2, y: 2, z: 4, core: 2. Of those that a mesh axis runs over, the one named last changes fastest.
Arguments:
- hidden_in: bfloat16 [256, 3584], P(('groups', 'expert')), may hold values from -6 to 6
- batch_len: int32 [1], P('groups'), may hold values from 64 to 256
- expert_ids: int32 [256, 8], P(('groups', 'expert')), may hold values from 0 to 15, all different within a row; in each aligned block of 16 rows (0 to 15, 16 to 31, ...) at most 12 rows name the same one
- gate_num: int32 [256, 8], P(('groups', 'expert')), may hold values from 1 to 1024
- w_gate: bfloat16 [16, 3584, 1024], P('expert', None, 'tensor'), may hold values from -0.09375 to 0.09375
- w_up: bfloat16 [16, 3584, 1024], P('expert', None, 'tensor'), may hold values from -0.09375 to 0.09375
- w_down: bfloat16 [16, 1024, 3584], P('expert', 'tensor'), may hold values from -0.1875 to 0.1875
- q_latent: bfloat16 [2, 64, 512], P('groups', 'tensor'), may hold values from -117 to 117
- q_rope: bfloat16 [2, 64, 64], P('groups', 'tensor'), may hold values from -6 to 6
- kv_latent: bfloat16 [2, 2048, 512], P('groups', 'expert'), may hold values from -4 to 4
- kv_rope: bfloat16 [2, 64, 2048], P('groups', None, 'expert'), may hold values from -4 to 4
- ctx_len: int32 [2], P('groups'), may hold values from 1 to 2048, as said below
Outputs:
- moe_out: bfloat16 [256, 3584], P(('groups', 'expert'))
- attn_out: bfloat16 [2, 64, 512], P('groups', 'tensor')
Inputs may be any that keep to these rules, and one draw needn't show every extreme that they name: `expert_ids`: each row names 8 different experts; the 16 rows of one index of the expert axis name any one expert at most 12 times. `batch_len`: the live slots are the first ones of the replica. `ctx_len`: the first request's context fills all 2048 positions.
All inputs are finite; a program needn't handle non-finite values.
Results may differ from a plain program's by a relative error of at most 0.0028.
The roundings to bfloat16 on the way count: a program that leaves them out, or rounds other values in their place, can miss the bound.
Values may be sent and summed in bfloat16 or wider, within the bound.
A program may use at most 64 MiB of HBM per device.

v0:
```python
import jax
import jax.numpy as jnp
from jax import lax
from jax.sharding import PartitionSpec as P

gate_denominator = 1024.0
softmax_scale = 192.0 ** (-0.5)


def joined(value, axis, join):
    pieces = jax.tree.map(lambda part: lax.all_gather(part, axis), value)
    head = jax.tree.map(lambda part: part[0], pieces)
    tail = jax.tree.map(lambda part: part[1:], pieces)
    so_far, _ = lax.scan(lambda so_far, slab: (join(so_far, slab), None), head, tail)
    return so_far


def join_parts(first, second):
    peak = jnp.maximum(first[0], second[0])
    left = jnp.exp(first[0] - peak)
    right = jnp.exp(second[0] - peak)
    total = first[1] * left + second[1] * right
    weighted = first[2] * left[..., None] + second[2] * right[..., None]
    return (peak, total, weighted)


def local(
    hidden_in,
    batch_len,
    expert_ids,
    gate_num,
    w_gate,
    w_up,
    w_down,
    q_latent,
    q_rope,
    kv_latent,
    kv_rope,
    ctx_len,
):
    owners = lax.axis_size("expert")
    tok_rows, width = hidden_in.shape
    topk = expert_ids.shape[1]
    capacity = min(tok_rows, max(2, 3 * tok_rows * topk // (2 * owners)))
    first_row = lax.axis_index("expert") * tok_rows
    live = first_row + jnp.arange(tok_rows, dtype=jnp.int32) < batch_len[0]
    flat_expert = expert_ids.reshape(-1)
    live_pick = jnp.repeat(live, topk)
    onehot = (
        (flat_expert[:, None] == jnp.arange(owners, dtype=jnp.int32)[None, :]) & live_pick[:, None]
    ).astype(jnp.int32)
    ranking = jnp.cumsum(onehot, axis=0) - 1
    slot = jnp.sum(onehot * ranking, axis=1)
    target = jnp.where(live_pick, flat_expert * capacity + slot, owners * capacity)
    half_width = width // lax.axis_size("tensor")
    source = lax.dynamic_slice_in_dim(
        hidden_in, lax.axis_index("tensor") * half_width, half_width, 1
    )
    picked = jnp.repeat(source, topk, axis=0)
    packed = (
        jnp.zeros((owners * capacity, source.shape[1]), jnp.bfloat16)
        .at[target]
        .set(picked, mode="drop")
    )
    packed = packed.reshape(owners, capacity, source.shape[1])
    rows = lax.all_to_all(packed, "expert", split_axis=0, concat_axis=0, tiled=True)
    rows = lax.all_gather(rows, "tensor", axis=2, tiled=True)
    count = rows.shape[1]
    flat = rows.reshape(-1, width)
    gate = jnp.dot(flat, w_gate[0], preferred_element_type=jnp.float32)
    upper = jnp.dot(flat, w_up[0], preferred_element_type=jnp.float32)
    hidden = (jax.nn.silu(gate) * upper).astype(jnp.bfloat16)
    partial_value = jnp.dot(hidden, w_down[0], preferred_element_type=jnp.float32).reshape(
        owners, count, width
    )
    weight = jnp.where(live_pick, gate_num.reshape(-1).astype(jnp.float32) / gate_denominator, 0.0)
    back_index = jnp.where(live_pick, target, 0)
    whole = lax.psum(partial_value, "tensor").astype(jnp.bfloat16)
    back = lax.all_to_all(whole, "expert", split_axis=0, concat_axis=0, tiled=True)
    rows = back.reshape(owners * capacity, back.shape[2])[back_index].astype(jnp.float32)
    scaled = (rows * weight[:, None]).reshape(tok_rows, topk, back.shape[2])
    moe_out = jnp.sum(scaled, axis=1).astype(jnp.bfloat16)
    ctx_dev = kv_latent.shape[1]
    position = lax.axis_index("expert") * ctx_dev + jnp.arange(ctx_dev, dtype=jnp.int32)
    valid_pos = position[None, :] < ctx_len[:, None]
    scores = jnp.einsum("bhl,bpl->bhp", q_latent, kv_latent, preferred_element_type=jnp.float32)
    scores = scores + jnp.einsum(
        "bhr,brp->bhp", q_rope, kv_rope, preferred_element_type=jnp.float32
    )
    scores = jnp.where(valid_pos[:, None, :], scores * softmax_scale, -1e30)
    peak = jnp.max(scores, axis=2)
    probs = jnp.where(valid_pos[:, None, :], jnp.exp(scores - peak[..., None]), 0.0)
    total = jnp.sum(probs, axis=2)
    weighted = jnp.einsum(
        "bhp,bpl->bhl", probs.astype(jnp.bfloat16), kv_latent, preferred_element_type=jnp.float32
    )
    peak, total, weighted = joined((peak, total, weighted), "expert", join_parts)
    attn_out = (weighted / total[..., None]).astype(jnp.bfloat16)
    return (moe_out, attn_out)


def solution(mesh):
    return jax.shard_map(
        local,
        mesh=mesh,
        in_specs=(
            P(("groups", "expert"), None),
            P("groups"),
            P(("groups", "expert"), None),
            P(("groups", "expert"), None),
            P("expert", None, "tensor"),
            P("expert", None, "tensor"),
            P("expert", "tensor", None),
            P("groups", "tensor", None),
            P("groups", "tensor", None),
            P("groups", "expert", None),
            P("groups", None, "expert"),
            P("groups"),
        ),
        out_specs=(P(("groups", "expert"), None), P("groups", "tensor", None)),
        check_vma=False,
    )
```

profile of v0, /device:TPU:15, one launch (start us, length us, event | category | flops | bytes accessed | tf_op | source)
XLA Modules:
  0.0 198.9 jit_solution(3794449205425740436)
XLA Ops:
  7.2 0.0 copy-start
  7.2 0.0 all-gather.8.cloned.1.call-start
  7.2 0.7 broadcast_multiply_fusion
  8.0 0.8 copy.29
  9.4 0.1 broadcast_in_dim.49.clone
  9.5 0.1 reshape.142
  9.6 0.1 and.12
  9.7 0.1 copy.28
  9.7 0.1 mul.79
  9.8 0.1 eq.15
  9.9 0.1 fusion.24
  10.0 0.2 reduce_window_sum.11
  10.2 0.2 select_reduce_fusion
  10.4 0.8 constant_dynamic-slice_fusion.1
  11.2 1.5 scatter_custom_fusion
  12.7 0.0 copy-start.3
  12.7 0.0 copy-start.4
  12.8 0.2 reshape.144
  12.9 27.7 %all_to_all.10 = bf16[16,12,1792]{2,1,0:T(8,128)(2,1)} all-to-all(bf16[16,12,1792]{2,1,0:T(8,128)(2,1)S(1)} %reshape.144), channel_id=1, replica_groups=mesh['groups'=1,'expert'=16,'tensor'=2] {'expert'}, dimensions={0} | all-to-all | bytes 1376256 | tf_op jit(solution)/shard_map/all_to_all | solution.py:66
  40.6 0.0 all-gather.8.cloned.1.call-update
  40.6 0.0 all-gather.10.cloned.1.call-start
  40.7 0.1 broadcast_compare_fusion
  40.8 0.2 fusion.38
  41.0 0.0 copy-done.5
  41.0 0.2 fusion.37
  41.2 0.9 fusion.27
  42.1 0.0 all-gather.10.cloned.1.call-update
  42.1 0.2 fusion.26
  42.3 21.3 %all-gather.3 = f32[16,2,32]{2,1,0:T(2,128)S(1)} all-gather(f32[1,2,32]{2,1,0:T(2,128)S(1)} %bitcast.68), channel_id=2, replica_groups=mesh['groups'=1,'expert'=16,'tensor'=2] {'expert'}, dimensions={0}, use_global_device_ids=true | all-gather | bytes 4352 | tf_op jit(solution)/shard_map/all_gather | solution.py:11
  63.6 31.6 %all-gather.4 = f32[16,2,32]{2,1,0:T(2,128)S(1)} all-gather(f32[1,2,32]{2,1,0:T(2,128)S(1)} %bitcast.69), channel_id=3, replica_groups=mesh['groups'=1,'expert'=16,'tensor'=2] {'expert'}, dimensions={0}, use_global_device_ids=true | all-gather | bytes 4352 | tf_op jit(solution)/shard_map/all_gather | solution.py:11
  95.3 0.1 copy.33
  95.3 2.4 %reshape.145 = bf16[192,3584]{1,0:T(8,128)(2,1)S(1)} reshape(bf16[16,12,3584]{2,1,0:T(8,128)(2,1)} %all-gather.8.cloned.1.call-done) | data formatting | bytes 2752512 | tf_op jit(solution)/shard_map/reshape | solution.py:69
  97.7 3.1 %fusion.7 = f32[192,512]{1,0:T(8,128)S(1)} fusion(bf16[192,3584]{1,0:T(8,128)(2,1)S(1)} %reshape.145, bf16[1,3584,512]{2,1,0:T(8,128)(2,1)} %param.18), kind=kOutput, calls=%fused_computation.15 | convolution fusion | flops 704643072 | bytes 5439488 | tf_op jit(solution)/shard_map/dot_general | solution.py:70
  100.8 0.3 copy-done.7
  101.1 0.9 fusion.13
  102.1 3.0 %fusion.3 = f32[16,12,3584]{2,0,1:T(8,128)S(1)} fusion(bf16[1,512,3584]{2,1,0:T(8,128)(2,1)} %param.20, bf16[16,12,512]{2,1,0:T(8,128)(2,1)S(1)} %dot_general.22), kind=kOutput, calls=%fused_computation.11 | convolution fusion | flops 704643072 | bytes 6619136 | tf_op jit(solution)/shard_map/dot_general | solution.py:73
  105.0 25.2 %all-reduce.1 = bf16[16,12,3584]{2,0,1:T(8,128)(2,1)} all-reduce(f32[16,12,3584]{2,0,1:T(8,128)S(1)} %fusion.3), channel_id=1, replica_groups=mesh['groups'=1,'expert'=16,'tensor'=2] {'tensor'}, use_global_device_ids=true, to_apply=%region_3.4 | all-reduce | flops 688128 | bytes 4128768 | tf_op jit(solution)/shard_map/psum | solution.py:78
  130.2 3.4 %copy.32 = bf16[16,12,3584]{2,1,0:T(8,128)(2,1)} copy(bf16[16,12,3584]{2,0,1:T(8,128)(2,1)} %all-reduce.1) | data formatting | bytes 2752512 | tf_op jit(solution)/shard_map/convert_element_type | solution.py:78
  133.6 13.1 %all-to-all-start.1 = ((bf16[16,12,3584]{2,1,0:T(8,128)(2,1)}), bf16[16,12,3584]{2,1,0:T(8,128)(2,1)S(1)}, u32[]{:S(2)}, u32[]{:S(2)}) async-start(bf16[16,12,3584]{2,1,0:T(8,128)(2,1)} %copy.32), calls=%async_computation.1 | async-start | bytes 3670016 | tf_op jit(solution)/shard_map/all_to_all | solution.py:79
  146.7 0.0 all-gather.10.cloned.1.call-done
  146.8 0.0 slice-start.1
  146.8 0.0 slice-start.2
  146.8 3.1 %slice.41 = f32[30,32,512]{2,1,0:T(8,128)} slice(f32[32,32,512]{2,1,0:T(8,128)} %all-gather.10.cloned.1.call-done), slice={[2:32], [0:32], [0:512]} | slice | bytes 3932160 | tf_op jit(solution)/shard_map/slice | solution.py:13
  149.9 15.7 %while.14 = (s32[]{:T(128)}, f32[2,32]{1,0:T(2,128)S(1)}, f32[2,32]{1,0:T(2,128)S(1)}, f32[2,32,512]{2,1,0:T(8,128)S(1)}, f32[15,2,32]{2,1,0:T(2,128)S(1)}, /*in...) while((s32[]{:T(128)}, f32[2,32]{1,0:T(2,128)S(1)}, f32[2,32]{1,0:T(2,128)S(1)}, ...), condition=%wide.region_8.9_spmd, body=%wide.region_7.8_spmd.sunk | while | flops 98690 | bytes 395877 | solution.py:14
  150.0 1.0 fusion.49
  151.0 1.0 fusion.49
  152.1 1.0 fusion.49
  153.1 1.0 fusion.49
  154.2 1.0 fusion.49
  155.2 1.0 fusion.49
  156.2 1.0 fusion.49
  157.3 1.0 fusion.49
  158.3 1.0 fusion.49
  159.4 1.0 fusion.49
  160.4 1.0 fusion.49
  161.5 1.0 fusion.49
  162.5 1.0 fusion.49
  163.6 1.0 fusion.49
  164.6 1.0 fusion.49
  165.6 0.7 divide_convert_fusion
  166.3 22.9 %all-to-all-done.1 = bf16[16,12,3584]{2,1,0:T(8,128)(2,1)S(1)} async-done(((bf16[16,12,3584]{2,1,0:T(8,128)(2,1)}), bf16[16,12,3584]{2,1,0:T(8,128)(2,1)S(1)}, u32[]{:S(2)}, u32[]{:S(2)}) %all-to-all-start.1) | async-done | bytes 1376288 | tf_op jit(solution)/shard_map/all_to_all | solution.py:79
  189.2 0.3 reshape.146
  189.6 1.1 gather_fusion
  190.7 1.3 fusion.9
  (41 shorter events, 0.5 us)
Async XLA Ops:
  7.2 33.6 %copy-start = (bf16[2,128,512]{2,1,0:T(8,128)(2,1)S(1)}, bf16[2,128,512]{2,1,0:T(8,128)(2,1)}, u32[]{:S(2)}) copy-start(bf16[2,128,512]{2,1,0:T(8,128)(2,1)} %param.23) | copy-start | bytes 786436
  7.2 88.2 %all-gather.8.cloned.1.call-start = ((), (), s32[]{:S(2)}) async-start(), calls=%async_computation.2 | async-start | bytes 2752512 | tf_op jit(solution)/shard_map/all_gather | solution.py:67
  12.7 28.0 %copy-start.8 = (s32[2]{0:T(128)S(1)}, s32[2]{0:T(128)}, u32[]{:S(2)}) copy-start(s32[2]{0:T(128)} %param.25) | copy-start | bytes 28
  12.7 28.1 %copy-start.3 = (bf16[2,32,512]{2,1,0:T(8,128)(2,1)S(1)}, bf16[2,32,512]{2,1,0:T(8,128)(2,1)}, u32[]{:S(2)}) copy-start(bf16[2,32,512]{2,1,0:T(8,128)(2,1)} %param.21) | copy-start | bytes 196612
  12.7 28.2 %copy-start.4 = (bf16[2,64,128]{2,1,0:T(8,128)(2,1)S(1)}, bf16[2,64,128]{2,1,0:T(8,128)(2,1)}, u32[]{:S(2)}) copy-start(bf16[2,64,128]{2,1,0:T(8,128)(2,1)} %param.24) | copy-start | bytes 98308
  12.7 28.2 %copy-start.5 = (bf16[2,32,64]{2,1,0:T(8,128)(2,1)S(1)}, bf16[2,32,64]{2,1,0:T(8,128)(2,1)}, u32[]{:S(2)}) copy-start(bf16[2,32,64]{2,1,0:T(8,128)(2,1)} %param.22) | copy-start | bytes 24580
  12.9 82.3 %copy-start.6 = (s32[16,8]{0,1:T(8,128)S(1)}, s32[16,8]{0,1:T(8,128)}, u32[]{:S(2)}) copy-start(s32[16,8]{0,1:T(8,128)} %param.17) | copy-start | bytes 1540
  40.6 106.1 %all-gather.10.cloned.1.call-start = ((), (), s32[]{:S(2)}) async-start(), calls=%async_computation.3 | async-start | bytes 2228224 | tf_op jit(solution)/shard_map/all_gather | solution.py:11
  63.6 37.2 %copy-start.1 = (f32[16,2,32]{2,1,0:T(2,128)}, f32[16,2,32]{2,1,0:T(2,128)S(1)}, u32[]{:S(2)}) copy-start(f32[16,2,32]{2,1,0:T(2,128)S(1)} %all-gather.3) | copy-start | bytes 12292
  95.2 5.6 %copy-start.2 = (f32[16,2,32]{2,1,0:T(2,128)}, f32[16,2,32]{2,1,0:T(2,128)S(1)}, u32[]{:S(2)}) copy-start(f32[16,2,32]{2,1,0:T(2,128)S(1)} %all-gather.4) | copy-start | bytes 12292
  97.7 3.4 %copy-start.7 = (bf16[1,3584,512]{2,1,0:T(8,128)(2,1)S(1)}, bf16[1,3584,512]{2,1,0:T(8,128)(2,1)}, u32[]{:S(2)}) copy-start(bf16[1,3584,512]{2,1,0:T(8,128)(2,1)} %param.19) | copy-start | bytes 11010052
  133.6 55.6 %all-to-all-start.1 = ((bf16[16,12,3584]{2,1,0:T(8,128)(2,1)}), bf16[16,12,3584]{2,1,0:T(8,128)(2,1)S(1)}, u32[]{:S(2)}, u32[]{:S(2)}) async-start(bf16[16,12,3584]{2,1,0:T(8,128)(2,1)} %copy.32), calls=%async_computation.1 | async-start | bytes 3670016 | tf_op jit(solution)/shard_map/all_to_all | solution.py:79
  146.7 3.2 %slice-start = ((f32[32,32,512]{2,1,0:T(8,128)}), f32[2,32,512]{2,1,0:T(8,128)S(1)}, s32[]{:S(2)}) async-start(f32[32,32,512]{2,1,0:T(8,128)} %all-gather.10.cloned.1.call-done), calls=%async_computation.4 | async-start | bytes 262144 | tf_op jit(solution)/shard_map/slice | solution.py:12
  146.8 3.2 %slice-start.1 = ((f32[16,2,32]{2,1,0:T(2,128)}), f32[15,2,32]{2,1,0:T(2,128)S(1)}, s32[]{:S(2)}) async-start(f32[16,2,32]{2,1,0:T(2,128)} %copy-done.1), calls=%async_computation.5 | async-start | bytes 30720 | tf_op jit(solution)/shard_map/slice | solution.py:13
  146.8 3.2 %slice-start.2 = ((f32[16,2,32]{2,1,0:T(2,128)}), f32[15,2,32]{2,1,0:T(2,128)S(1)}, s32[]{:S(2)}) async-start(f32[16,2,32]{2,1,0:T(2,128)} %copy-done.2), calls=%async_computation.6 | async-start | bytes 30720 | tf_op jit(solution)/shard_map/slice | solution.py:13
Sparse Core Ops, SparseCore 0:
  40.7 11.6 all-gather.7
  55.2 59.0 all-gather.9
where the time goes:
time: 200 us; the launch traced here: 199 us
  blocking collectives  106 us (53%)
  waiting for transfers between devices  22.9 us (11%)
  other arithmetic  18.9 us (9%)
  between operations  15 us (8%)
  local copies, waits for them, and re-layouts  14.6 us (7%)
  starting transfers between devices  13.2 us (7%)
  matrix products  8.19 us (4%)
    all_gather x2, blocking collectives, joined(): pieces = jax.tree.map(lambda part: lax.all_gather(part, axis), value)  52.9 us
    all_to_all x1, blocking collectives, local(): lax.all_to_all(packed, 'expert', split_axis=0, concat_axis=0, tiled=True)  27.7 us
    psum x1, blocking collectives, local(): whole = lax.psum(partial_value, 'tensor').astype(jnp.bfloat16)  25.2 us
    all_to_all x1, waiting for transfers between devices, local(): lax.all_to_all(whole, 'expert', split_axis=0, concat_axis=0, tiled=True)  22.9 us
    add x15, other arithmetic, join_parts(): weighted = first[2] * left[..., None] + second[2] * right[..., None]  15 us
    all_to_all x1, starting transfers between devices, local(): lax.all_to_all(whole, 'expert', split_axis=0, concat_axis=0, tiled=True)  13.1 us
  transfers between devices with their start and end apart: 3, of which 1 were waited for; matrix products, arithmetic and copies ran while one was open for 17% of the time, Pallas kernels for 0%

commit v1 on v0

v1 whole, which is shorter than its diff:
```python
import functools

import jax
import jax.numpy as jnp
from jax import lax
from jax.experimental import pallas as pl
from jax.experimental.pallas import tpu as pltpu
from jax.sharding import PartitionSpec as P

gate_denominator = 1024.0
softmax_scale = 192.0 ** (-0.5)
LANES = 128
SUB = 8
F32 = jnp.float32
BF16 = jnp.bfloat16


def iota(shape, dim):
    return lax.broadcasted_iota(jnp.int32, shape, dim)


def remote(src, dst, send, recv, **where):
    return pltpu.make_async_remote_copy(
        src_ref=src,
        dst_ref=dst,
        send_sem=send,
        recv_sem=recv,
        device_id=where,
        device_id_type=pl.DeviceIdType.MESH,
    )


def kernel(
    n,
    full,
    fold,
    chunks,
    x_hbm,
    blen,
    ids,
    gnum,
    wg_hbm,
    wu_hbm,
    wd_hbm,
    ql,
    qr,
    kvl_hbm,
    kvr_hbm,
    clen,
    moe_out,
    attn_out,
    xb,
    xp,
    wg,
    wu,
    wd,
    kvl,
    kvr,
    hid,
    val,
    ret,
    aps,
    apr,
    ares,
    ob,
    op,
    local_sem,
    col_recv,
    x_recv,
    y_recv,
    d_recv,
    send_sem,
    recv_sem,
):
    me = lax.axis_index("expert")
    core = lax.axis_index("tensor")
    other = 1 - core
    rows, width = x_hbm.shape
    half = width // 2
    quarter = half // 2
    topk = ids.shape[1]
    outer = n // 4
    tokens = n * rows
    batch, heads, lat = ql.shape
    mine = pl.ds(pl.multiple_of(core * half, LANES), half)
    theirs = pl.ds(pl.multiple_of(other * half, LANES), half)

    x_load = pltpu.make_async_copy(
        x_hbm.at[:, mine], xb.at[me, :, pl.ds(LANES, half)], local_sem.at[0]
    )
    x_load.start()
    kv_loads = [
        pltpu.make_async_copy(kvl_hbm, kvl, local_sem.at[1]),
        pltpu.make_async_copy(kvr_hbm, kvr, local_sem.at[2]),
    ]
    for copy in kv_loads:
        copy.start()
    mine_rows = pl.ds(pl.multiple_of(core * half, LANES), half)
    their_rows = pl.ds(pl.multiple_of(other * half, LANES), half)
    w_loads = [
        pltpu.make_async_copy(wg_hbm.at[0, mine_rows], wg.at[0], local_sem.at[3]),
        pltpu.make_async_copy(wu_hbm.at[0, mine_rows], wu.at[0], local_sem.at[4]),
        pltpu.make_async_copy(wg_hbm.at[0, their_rows], wg.at[1], local_sem.at[5]),
        pltpu.make_async_copy(wu_hbm.at[0, their_rows], wu.at[1], local_sem.at[6]),
        pltpu.make_async_copy(wd_hbm.at[0, :, mine], wd.at[core], local_sem.at[7]),
    ]

    barrier = pltpu.get_barrier_semaphore()

    def greet(step, carry):
        pl.semaphore_signal(
            barrier,
            inc=1,
            device_id={"expert": lax.rem(me + step, n)},
            device_id_type=pl.DeviceIdType.MESH,
        )
        return carry

    lax.fori_loop(1, n, greet, 0)
    pl.semaphore_signal(
        barrier, inc=1, device_id={"tensor": other}, device_id_type=pl.DeviceIdType.MESH
    )

    live = (me * rows + iota((rows, LANES), 0)) < blen[0]
    lane = iota((rows, LANES), 1)
    named = jnp.zeros((rows, LANES), F32)
    gates = jnp.zeros((rows, LANES), jnp.int32)
    for k in range(topk):
        hit = (ids[:, k : k + 1] == lane) & live
        named = named + jnp.where(hit, 1.0, 0.0)
        gates = gates + jnp.where(hit, gnum[:, k : k + 1], 0)
    below = jnp.where(iota((rows, rows), 1) < iota((rows, rows), 0), 1.0, 0.0).astype(BF16)
    rank = jnp.dot(below, named.astype(BF16), preferred_element_type=F32)
    code = jnp.where(named > 0.5, rank + 1.0, 0.0)
    xb[me, :, 0:LANES] = code.astype(BF16)

    x_load.wait()
    pl.semaphore_wait(barrier, n)

    bit_x = lax.rem(me, 2)
    bit_y = lax.rem(me // 2, 2)
    plane = me - 2 * bit_y - bit_x
    spot = 2 * bit_y + bit_x
    group = me // 4
    x_side = me + 1 - 2 * bit_x
    y_side = me + 2 - 4 * bit_y
    x_spot = spot + 1 - 2 * bit_x
    y_spot = spot + 2 - 4 * bit_y
    d_spot = 3 - spot
    cuts = (pl.ds(0, LANES + quarter), pl.ds(LANES + quarter, quarter))
    feats = (pl.ds(LANES, quarter), pl.ds(LANES + quarter, quarter))
    lands = (pl.ds(0, quarter), pl.ds(quarter, quarter))

    def block_of(step, place):
        return lax.rem(group - step + outer, outer) * 4 + place

    def to_core(block, h):
        remote(
            xb.at[block, :, feats[h]],
            xp.at[block, :, lands[h]],
            send_sem.at[0],
            recv_sem.at[0],
            tensor=other,
        ).start()

    def to_x(block, h, recv):
        part = xb.at[block, :, cuts[h]]
        remote(part, part, send_sem.at[1], recv, expert=x_side).start()

    def to_y(block, h, recv):
        part = xb.at[block, :, cuts[h]]
        remote(part, part, send_sem.at[2], recv, expert=y_side).start()

    def landed(block, h, recv):
        part = xb.at[block, :, cuts[h]]
        remote(part, part, send_sem.at[3], recv, expert=x_side).wait_recv()

    for h in range(2):
        to_x(me, h, x_recv.at[0, h])
        to_y(me, h, y_recv.at[0, h])
        for step in range(1, outer):
            part = xb.at[me, :, cuts[h]]
            remote(
                part,
                part,
                send_sem.at[3],
                col_recv.at[step, h],
                expert=lax.rem(group + step, outer) * 4 + spot,
            ).start()
    for h in range(2):
        to_core(me, h)
    for copy in w_loads:
        copy.start()
    w_swap = remote(
        wd_hbm.at[0, :, theirs], wd.at[core], send_sem.at[4], recv_sem.at[1], tensor=other
    )
    w_swap.start()

    for copy in kv_loads:
        copy.wait()
    positions = kvl.shape[1]
    where_p = me * positions + iota((heads, positions), 1)
    parts = lat * SUB * chunks // (batch * heads * lat)
    part_w = lat // parts
    per_batch = heads // SUB
    for b in range(batch):
        valid = where_p < clen[b]
        scores = lax.dot_general(
            ql[b], kvl[b], (((1,), (1,)), ((), ())), preferred_element_type=F32
        )
        scores = scores + jnp.dot(qr[b], kvr[b], preferred_element_type=F32)
        scores = jnp.where(valid, scores * softmax_scale, -1e30)
        peak = jnp.max(scores, axis=1, keepdims=True)
        probs = jnp.where(valid, jnp.exp(scores - peak), 0.0)
        total = jnp.sum(probs, axis=1, keepdims=True)
        weighted = jnp.dot(probs.astype(BF16), kvl[b], preferred_element_type=F32)
        both = jnp.where(iota((heads, LANES), 1) < LANES // 2, peak, total)
        for g in range(per_batch):
            rs = slice(g * SUB, (g + 1) * SUB)
            for c in range(parts):
                at = (b * per_batch + g) * parts + c
                aps[at, :, 0:part_w] = weighted[rs, c * part_w : (c + 1) * part_w]
                aps[at, :, part_w : part_w + LANES] = both[rs]

    def share(step, carry):
        dest = lax.rem(me + step, n)

        @pl.when(dest < chunks)
        def _():
            remote(
                aps.at[dest], apr.at[me], send_sem.at[5], recv_sem.at[2], expert=dest
            ).start()

        return carry

    lax.fori_loop(1, n, share, 0)

    for step in range(outer):
        if step + 1 < outer:
            block = block_of(step + 1, spot)
            for h in range(2):
                landed(block, h, col_recv.at[step + 1, h])
                to_x(block, h, x_recv.at[step + 1, h])
                to_y(block, h, y_recv.at[step + 1, h])
                to_core(block, h)
        from_x, from_y = block_of(step, x_spot), block_of(step, y_spot)
        landed(from_x, 0, x_recv.at[step, 0])
        to_y(from_x, 0, d_recv.at[step, 0])
        to_core(from_x, 0)
        landed(from_y, 0, y_recv.at[step, 0])
        to_core(from_y, 0)
        landed(from_y, 1, y_recv.at[step, 1])
        to_x(from_y, 1, d_recv.at[step, 1])
        to_core(from_y, 1)
        landed(from_x, 1, x_recv.at[step, 1])
        to_core(from_x, 1)
    for step in range(outer):
        block = block_of(step, d_spot)
        for h in range(2):
            landed(block, h, d_recv.at[step, h])
            to_core(block, h)

    seen = jnp.where(iota((SUB, LANES), 1) == me, 1.0, 0.0).astype(BF16)
    codes = xb[:, :, 0:LANES].reshape(tokens, LANES)
    code_row = lax.dot_general(
        seen, codes, (((1,), (1,)), ((), ())), preferred_element_type=F32
    )[0:1]
    groups = full + fold
    packs = []
    for g in range(groups):
        r = iota((n * SUB, tokens), 0)
        j = r % SUB
        slot = g * SUB + (j if g < full else j % (SUB // 2))
        same = (r // SUB) == (iota((n * SUB, tokens), 1) // rows)
        hit = same & (code_row == (slot + 1).astype(F32))
        packs.append(jnp.where(hit, 1.0, 0.0).astype(BF16))
    pack = jnp.concatenate(packs, axis=0) if groups > 1 else packs[0]

    for copy in w_loads[:4]:
        copy.wait()
    x_own = xb[:, :, LANES:].reshape(tokens, half)
    gate = jnp.dot(x_own, wg[0], preferred_element_type=F32)
    upper = jnp.dot(x_own, wu[0], preferred_element_type=F32)
    remote(xp, xp, send_sem.at[0], recv_sem.at[0], tensor=other).wait_recv()
    x_other = xp[...].reshape(tokens, half)
    gate = gate + jnp.dot(x_other, wg[1], preferred_element_type=F32)
    upper = upper + jnp.dot(x_other, wu[1], preferred_element_type=F32)
    hidden = (gate / (1.0 + jnp.exp(-gate)) * upper).astype(BF16)
    hid[core] = hidden
    h_swap = remote(hid.at[core], hid.at[core], send_sem.at[6], recv_sem.at[3], tensor=other)
    h_swap.start()

    @pl.when(me < chunks)
    def _():
        remote(
            apr.at[pl.ds(0, n - 1)],
            apr.at[pl.ds(0, n - 1)],
            send_sem.at[5],
            recv_sem.at[2],
            expert=x_side,
        ).wait_recv()
        apr[me] = aps[me]
        peaks = apr[:, :, part_w : part_w + 1]
        totals = apr[:, :, part_w + LANES // 2 : part_w + LANES // 2 + 1]
        top = jnp.max(peaks, axis=0, keepdims=True)
        scale = jnp.exp(peaks - top)
        total = jnp.sum(totals * scale, axis=0)
        joined = jnp.sum(apr[:, :, 0:part_w] * scale, axis=0)
        ares[me] = (joined / total).astype(BF16)

        def tell(step, carry):
            remote(
                ares.at[me],
                ares.at[me],
                send_sem.at[7],
                recv_sem.at[4],
                expert=lax.rem(me + step, n),
            ).start()
            return carry

        lax.fori_loop(1, n, tell, 0)

    w_loads[4].wait()
    w_swap.wait_recv()
    own_packed = jnp.dot(pack, hid[core], preferred_element_type=F32).astype(BF16)
    value = jnp.dot(own_packed, wd[core], preferred_element_type=F32)
    h_swap.wait_recv()
    their_packed = jnp.dot(pack, hid[other], preferred_element_type=F32).astype(BF16)
    value = (value + jnp.dot(their_packed, wd[other], preferred_element_type=F32)).astype(BF16)
    left, right = value[:, :quarter], value[:, quarter:]
    for g in range(full):
        rs = slice(g * n * SUB, (g + 1) * n * SUB)
        val[:, 2 * g] = left[rs].reshape(n, SUB, quarter)
        val[:, 2 * g + 1] = right[rs].reshape(n, SUB, quarter)
    if fold:
        rs = slice(full * n * SUB, (full + 1) * n * SUB)
        low = iota((n * SUB, quarter), 0) % SUB < SUB // 2
        val[:, 2 * full] = jnp.where(low, left[rs], right[rs]).reshape(n, SUB, quarter)

    def give(step, carry):
        dest = lax.rem(me + step, n)
        remote(val.at[dest], ret.at[me], send_sem.at[8], recv_sem.at[5], expert=dest).start()
        return carry

    lax.fori_loop(1, n, give, 0)
    ret[me] = val[me]

    high = gates // 16 * 16
    spread_in = jnp.concatenate(
        [high.astype(F32), (gates - high).astype(F32), code], axis=0
    ).astype(BF16)
    spot_of = jnp.where(
        iota((LANES, n * SUB), 0) == iota((LANES, n * SUB), 1) // SUB, 1.0, 0.0
    ).astype(BF16)
    spread = jnp.dot(spread_in, spot_of, preferred_element_type=F32)
    weights = spread[: 2 * rows]
    codes_r = spread[2 * rows :]
    codes_r = jnp.concatenate([codes_r, codes_r], axis=0)
    j = iota((2 * rows, n * SUB), 1) % SUB
    mats = []
    for g in range(full):
        hit = codes_r == (g * SUB + j + 1).astype(F32)
        mats.append(jnp.where(hit, weights, 0.0).astype(BF16))
    if fold:
        hit = codes_r == (full * SUB + j % (SUB // 2) + 1).astype(F32)
        for low in (True, False):
            side = (j < SUB // 2) if low else (j >= SUB // 2)
            mats.append(jnp.where(hit & side, weights, 0.0).astype(BF16))

    @pl.when(me < chunks)
    def _():
        part = ares.at[pl.ds(0, chunks - 1)]
        remote(part, part, send_sem.at[7], recv_sem.at[4], expert=x_side).wait_recv()

    if chunks < n:

        @pl.when(me >= chunks)
        def _():
            remote(ares, ares, send_sem.at[7], recv_sem.at[4], expert=x_side).wait_recv()

    for b in range(batch):
        for g in range(per_batch):
            for c in range(parts):
                at = (b * per_batch + g) * parts + c
                attn_out[b, g * SUB : (g + 1) * SUB, c * part_w : (c + 1) * part_w] = ares[at]

    remote(xp, xp, send_sem.at[0], recv_sem.at[0], tensor=other).wait_send()
    for sem in (1, 2):
        part = xb.at[pl.ds(0, outer)]
        remote(part, part, send_sem.at[sem], recv_sem.at[0], expert=x_side).wait_send()
    for h in range(outer):
        part = xb.at[h, :, cuts[0]]
        remote(part, part, send_sem.at[2], recv_sem.at[0], expert=x_side).wait_send()
        part = xb.at[h, :, cuts[1]]
        remote(part, part, send_sem.at[1], recv_sem.at[0], expert=x_side).wait_send()
    part = xb.at[pl.ds(0, outer - 1)]
    remote(part, part, send_sem.at[3], recv_sem.at[0], expert=x_side).wait_send()
    w_swap.wait_send()
    h_swap.wait_send()

    sent = chunks - jnp.where(me < chunks, 1, 0)

    def drain(step, carry):
        remote(aps.at[0], apr.at[0], send_sem.at[5], recv_sem.at[2], expert=x_side).wait_send()
        return carry

    lax.fori_loop(0, sent, drain, 0)

    @pl.when(me < chunks)
    def _():
        def drain_result(step, carry):
            remote(
                ares.at[0], ares.at[0], send_sem.at[7], recv_sem.at[4], expert=x_side
            ).wait_send()
            return carry

        lax.fori_loop(1, n, drain_result, 0)

    part = ret.at[pl.ds(0, n - 1)]
    remote(part, part, send_sem.at[8], recv_sem.at[5], expert=x_side).wait_recv()
    lo = jnp.zeros((2 * rows, quarter), F32)
    hi = jnp.zeros((2 * rows, quarter), F32)
    for g in range(full):
        lo = lo + jnp.dot(
            mats[g], ret[:, 2 * g].reshape(n * SUB, quarter), preferred_element_type=F32
        )
        hi = hi + jnp.dot(
            mats[g], ret[:, 2 * g + 1].reshape(n * SUB, quarter), preferred_element_type=F32
        )
    if fold:
        last = ret[:, 2 * full].reshape(n * SUB, quarter)
        lo = lo + jnp.dot(mats[full], last, preferred_element_type=F32)
        hi = hi + jnp.dot(mats[full + 1], last, preferred_element_type=F32)
    ob[:, :quarter] = ((lo[:rows] + lo[rows:]) / gate_denominator).astype(BF16)
    ob[:, quarter:] = ((hi[:rows] + hi[rows:]) / gate_denominator).astype(BF16)
    o_swap = remote(ob, op, send_sem.at[9], recv_sem.at[6], tensor=other)
    o_swap.start()
    moe_out[:, mine] = ob[...]
    remote(part, part, send_sem.at[8], recv_sem.at[5], expert=x_side).wait_send()
    o_swap.wait()
    moe_out[:, theirs] = op[...]


def local(
    hidden_in,
    batch_len,
    expert_ids,
    gate_num,
    w_gate,
    w_up,
    w_down,
    q_latent,
    q_rope,
    kv_latent,
    kv_rope,
    ctx_len,
):
    n = lax.axis_size("expert")
    rows, width = hidden_in.shape
    topk = expert_ids.shape[1]
    capacity = min(rows, max(2, 3 * rows * topk // (2 * n)))
    rest = capacity % SUB
    full = capacity // SUB + (1 if rest > SUB // 2 else 0)
    fold = 1 if 0 < rest <= SUB // 2 else 0
    half = width // 2
    hidden = w_gate.shape[2]
    batch, heads, lat = q_latent.shape
    row_groups = batch * heads // SUB
    chunks = row_groups * min(max(1, n // row_groups), lat // LANES)
    part_w = lat * row_groups // chunks
    parts_v = 2 * full + fold
    outer = n // 4
    anywhere = pl.BlockSpec(memory_space=pl.ANY)
    vmem = pl.BlockSpec(memory_space=pltpu.VMEM)
    smem = pl.BlockSpec(memory_space=pltpu.SMEM)
    return pl.pallas_call(
        functools.partial(kernel, n, full, fold, chunks),
        out_shape=(
            jax.ShapeDtypeStruct((rows, width), BF16),
            jax.ShapeDtypeStruct((batch, heads, lat), BF16),
        ),
        in_specs=[
            anywhere,
            smem,
            vmem,
            vmem,
            anywhere,
            anywhere,
            anywhere,
            vmem,
            vmem,
            anywhere,
            anywhere,
            smem,
        ],
        out_specs=(vmem, vmem),
        scratch_shapes=[
            pltpu.VMEM((n, rows, LANES + half), BF16),
            pltpu.VMEM((n, rows, half), BF16),
            pltpu.VMEM((2, half, hidden), BF16),
            pltpu.VMEM((2, half, hidden), BF16),
            pltpu.VMEM((2, hidden, half), BF16),
            pltpu.VMEM(kv_latent.shape, BF16),
            pltpu.VMEM(kv_rope.shape, BF16),
            pltpu.VMEM((2, n * rows, hidden), BF16),
            pltpu.VMEM((n, parts_v, SUB, half // 2), BF16),
            pltpu.VMEM((n, parts_v, SUB, half // 2), BF16),
            pltpu.VMEM((chunks, SUB, part_w + LANES), F32),
            pltpu.VMEM((n, SUB, part_w + LANES), F32),
            pltpu.VMEM((chunks, SUB, part_w), BF16),
            pltpu.VMEM((rows, half), BF16),
            pltpu.VMEM((rows, half), BF16),
            pltpu.SemaphoreType.DMA((8,)),
            pltpu.SemaphoreType.DMA((outer, 2)),
            pltpu.SemaphoreType.DMA((outer, 2)),
            pltpu.SemaphoreType.DMA((outer, 2)),
            pltpu.SemaphoreType.DMA((outer, 2)),
            pltpu.SemaphoreType.DMA((10,)),
            pltpu.SemaphoreType.DMA((7,)),
        ],
        compiler_params=pltpu.CompilerParams(
            collective_id=0, has_side_effects=True, vmem_limit_bytes=60 * 1024 * 1024
        ),
    )(
        hidden_in,
        batch_len,
        expert_ids,
        gate_num,
        w_gate,
        w_up,
        w_down,
        q_latent,
        q_rope,
        kv_latent,
        kv_rope,
        ctx_len,
    )


def solution(mesh):
    return jax.shard_map(
        local,
        mesh=mesh,
        in_specs=(
            P(("groups", "expert"), None),
            P("groups"),
            P(("groups", "expert"), None),
            P(("groups", "expert"), None),
            P("expert", None, "tensor"),
            P("expert", None, "tensor"),
            P("expert", "tensor", None),
            P("groups", "tensor", None),
            P("groups", "tensor", None),
            P("groups", "expert", None),
            P("groups", None, "expert"),
            P("groups"),
        ),
        out_specs=(P(("groups", "expert"), None), P("groups", "tensor", None)),
        check_vma=False,
    )
```

time: 200 us -> 55.3 us (0.28)
  blocking collectives: 106 us -> 0 us
  Pallas kernels: 0 us -> 48 us
  waiting for transfers between devices: 22.9 us -> 0 us
  other arithmetic: 18.9 us -> 0 us
  between operations: 15 us -> 1.29 us
  starting transfers between devices: 13.2 us -> 0 us
  local copies, waits for them, and re-layouts: 14.6 us -> 5.73 us
  matrix products: 8.19 us -> 0 us
    all_gather x2 -> x0, blocking collectives: 52.9 us -> none  [joined(): pieces = jax.tree.map(lambda part: lax.all_gather(part, axis), value)]
    pallas_call x0 -> x1, Pallas kernels: none -> 48 us  [local(): pl.pallas_call(functools.partial(kernel, n, full, fold, chunks), out_shap...]
    all_to_all x1 -> x0, blocking collectives: 27.7 us -> none  [local(): lax.all_to_all(packed, 'expert', split_axis=0, concat_axis=0, tiled=True)]
    psum x1 -> x0, blocking collectives: 25.2 us -> none  [local(): whole = lax.psum(partial_value, 'tensor').astype(jnp.bfloat16)]
    all_to_all x1 -> x0, waiting for transfers between devices: 22.9 us -> none  [local(): lax.all_to_all(whole, 'expert', split_axis=0, concat_axis=0, tiled=True)]
    add x31 -> x0, other arithmetic: 15.4 us -> none  [the longest x15 15 us: join_parts(): weighted = first[2] * left[..., None] + second[2] * right[..., None]]
    all_to_all x1 -> x0, starting transfers between devices: 13.1 us -> none  [local(): lax.all_to_all(whole, 'expert', split_axis=0, concat_axis=0, tiled=True)]
    dot_general x6 -> x0, matrix products: 8.19 us -> none  [the longest x1 3.08 us: local(): gate = jnp.dot(flat, w_gate[0], preferred_element_type=jnp.float32)]
  transfers between devices with their start and end apart: 3 -> 0, of which waited for: 1 -> 0; matrix products, arithmetic and copies ran while one was open for 17% -> 0% of each run, Pallas kernels for 0% -> 0%
where the time goes in v1:
time: 55.3 us; the launch traced here: 55 us
  Pallas kernels  48 us (87%)
  local copies, waits for them, and re-layouts  5.73 us (10%)
  between operations  1.29 us (2%)
    pallas_call x1, Pallas kernels, local(): pl.pallas_call(functools.partial(kernel, n, full, fold, chunks), out_shap...  48 us
    unnamed x4, local copies, waits for them, and re-layouts  5.73 us

profile of v1, /device:TPU:15, one launch (start us, length us, event | category | flops | bytes accessed | tf_op | source)
XLA Modules:
  0.0 55.0 jit_solution(13281784367752175393)
XLA Ops:
  1.3 1.4 %copy.14.ids = s32[16,8]{1,0:T(8,128)} copy(s32[16,8]{0,1:T(8,128)} %param.14) | data formatting | bytes 1024 | tf_op args[2]
  2.6 1.4 %copy.15.gnum = s32[16,8]{1,0:T(8,128)} copy(s32[16,8]{0,1:T(8,128)} %param.15) | data formatting | bytes 1024 | tf_op args[3]
  4.0 48.0 %shard_map.131 = (bf16[16,3584]{1,0:T(8,128)(2,1)}, bf16[2,32,512]{2,1,0:T(8,128)(2,1)}) custom-call(bf16[16,3584]{1,0:T(8,128)(2,1)} %x_hbm.1, s32[1]{0:T(128)S(6)} %copy.18.blen, s32[16,8]{1,0:T(8,128)} %copy.14.ids, s32[16,8]{1,0:T(8,128)} %copy.15.gnum, bf16[1,3584,512]{2,1,0:T(8,128)(2,1)} %wg_hbm.1, bf16[1,3584,512]{2,1,0:T(8,128)(2,1)} %wu_hbm.1, ...), custom_call_target="tpu_custom_call" | custom-call | tf_op jit(solution)/shard_map/pallas_call | solution.py:476
  52.0 1.6 %copy.19 = bf16[16,3584]{1,0:T(8,128)(2,1)} copy(bf16[16,3584]{1,0:T(8,128)(2,1)} %get-tuple-element.4) | data formatting | bytes 229376
  53.5 1.5 %copy.20 = bf16[2,32,512]{2,1,0:T(8,128)(2,1)} copy(bf16[2,32,512]{2,1,0:T(8,128)(2,1)} %get-tuple-element.5) | data formatting | bytes 131072

commit v2 on v1

--- a/solution.py
+++ b/solution.py
@@ -78,12 +78,16 @@
     rows, width = x_hbm.shape
     half = width // 2
     quarter = half // 2
-    topk = ids.shape[1]
+    topk = ids.shape[0]
     outer = n // 4
     tokens = n * rows
     batch, heads, lat = ql.shape
     mine = pl.ds(pl.multiple_of(core * half, LANES), half)
     theirs = pl.ds(pl.multiple_of(other * half, LANES), half)
+
+    order = [0] + sorted(range(1, outer), key=lambda step: -min(step, outer - step))
+    early = (outer + 1) // 2
+    stages = (order[:early], order[early:])
 
     x_load = pltpu.make_async_copy(
         x_hbm.at[:, mine], xb.at[me, :, pl.ds(LANES, half)], local_sem.at[0]
@@ -105,6 +109,9 @@
         pltpu.make_async_copy(wd_hbm.at[0, :, mine], wd.at[core], local_sem.at[7]),
     ]
 
+    for copy in w_loads:
+        copy.start()
+
     barrier = pltpu.get_barrier_semaphore()
 
     def greet(step, carry):
@@ -121,17 +128,26 @@
         barrier, inc=1, device_id={"tensor": other}, device_id_type=pl.DeviceIdType.MESH
     )
 
-    live = (me * rows + iota((rows, LANES), 0)) < blen[0]
-    lane = iota((rows, LANES), 1)
-    named = jnp.zeros((rows, LANES), F32)
-    gates = jnp.zeros((rows, LANES), jnp.int32)
+    live = (me * rows + iota((LANES, rows), 1)) < blen[0]
+    expert = iota((LANES, rows), 0)
+    named = jnp.zeros((LANES, rows), F32)
+    gates = jnp.zeros((LANES, rows), jnp.int32)
     for k in range(topk):
-        hit = (ids[:, k : k + 1] == lane) & live
+        hit = (ids[k : k + 1, :] == expert) & live
         named = named + jnp.where(hit, 1.0, 0.0)
-        gates = gates + jnp.where(hit, gnum[:, k : k + 1], 0)
-    below = jnp.where(iota((rows, rows), 1) < iota((rows, rows), 0), 1.0, 0.0).astype(BF16)
-    rank = jnp.dot(below, named.astype(BF16), preferred_element_type=F32)
-    code = jnp.where(named > 0.5, rank + 1.0, 0.0)
+        gates = gates + jnp.where(hit, gnum[k : k + 1, :], 0)
+    high = gates // 16 * 16
+    turn = (((1,), (1,)), ((), ()))
+    row, col = iota((rows, rows), 0), iota((rows, rows), 1)
+    below = jnp.where(col < row, 1.0, 0.0).astype(BF16)
+    same_row = jnp.where(col == row, 1.0, 0.0).astype(BF16)
+
+    def turned(left, right):
+        return lax.dot_general(left, right.astype(BF16), turn, preferred_element_type=F32)
+
+    code = jnp.where(turned(same_row, named) > 0.5, turned(below, named) + 1.0, 0.0)
+    gate_high = turned(same_row, high.astype(F32))
+    gate_low = turned(same_row, (gates - high).astype(F32))
     xb[me, :, 0:LANES] = code.astype(BF16)
 
     x_load.wait()
@@ -154,12 +170,12 @@
     def block_of(step, place):
         return lax.rem(group - step + outer, outer) * 4 + place
 
-    def to_core(block, h):
+    def to_core(block, h, stage):
         remote(
             xb.at[block, :, feats[h]],
             xp.at[block, :, lands[h]],
             send_sem.at[0],
-            recv_sem.at[0],
+            recv_sem.at[7 + stage],
             tensor=other,
         ).start()
 
@@ -178,7 +194,7 @@
     for h in range(2):
         to_x(me, h, x_recv.at[0, h])
         to_y(me, h, y_recv.at[0, h])
-        for step in range(1, outer):
+        for step in order[1:]:
             part = xb.at[me, :, cuts[h]]
             remote(
                 part,
@@ -188,9 +204,7 @@
                 expert=lax.rem(group + step, outer) * 4 + spot,
             ).start()
     for h in range(2):
-        to_core(me, h)
-    for copy in w_loads:
-        copy.start()
+        to_core(me, h, 0)
     w_swap = remote(
         wd_hbm.at[0, :, theirs], wd.at[core], send_sem.at[4], recv_sem.at[1], tensor=other
     )
@@ -222,6 +236,37 @@
                 aps[at, :, 0:part_w] = weighted[rs, c * part_w : (c + 1) * part_w]
                 aps[at, :, part_w : part_w + LANES] = both[rs]
 
+    def across(stage):
+        for step in stages[stage]:
+            block = block_of(step, d_spot)
+            for h in range(2):
+                landed(block, h, d_recv.at[step, h])
+                to_core(block, h, stage)
+
+    for at, step in enumerate(order):
+        if at + 1 < outer:
+            ahead = order[at + 1]
+            block = block_of(ahead, spot)
+            for h in range(2):
+                landed(block, h, col_recv.at[ahead, h])
+                to_x(block, h, x_recv.at[ahead, h])
+                to_y(block, h, y_recv.at[ahead, h])
+                to_core(block, h, 0 if at + 1 < early else 1)
+        stage = 0 if at < early else 1
+        from_x, from_y = block_of(step, x_spot), block_of(step, y_spot)
+        landed(from_x, 0, x_recv.at[step, 0])
+        to_y(from_x, 0, d_recv.at[step, 0])
+        to_core(from_x, 0, stage)
+        landed(from_y, 0, y_recv.at[step, 0])
+        to_core(from_y, 0, stage)
+        landed(from_y, 1, y_recv.at[step, 1])
+        to_x(from_y, 1, d_recv.at[step, 1])
+        to_core(from_y, 1, stage)
+        landed(from_x, 1, x_recv.at[step, 1])
+        to_core(from_x, 1, stage)
+        if at + 2 == outer:
+            across(0)
+
     def share(step, carry):
         dest = lax.rem(me + step, n)
 
@@ -235,120 +280,126 @@
 
     lax.fori_loop(1, n, share, 0)
 
-    for step in range(outer):
-        if step + 1 < outer:
-            block = block_of(step + 1, spot)
-            for h in range(2):
-                landed(block, h, col_recv.at[step + 1, h])
-                to_x(block, h, x_recv.at[step + 1, h])
-                to_y(block, h, y_recv.at[step + 1, h])
-                to_core(block, h)
-        from_x, from_y = block_of(step, x_spot), block_of(step, y_spot)
-        landed(from_x, 0, x_recv.at[step, 0])
-        to_y(from_x, 0, d_recv.at[step, 0])
-        to_core(from_x, 0)
-        landed(from_y, 0, y_recv.at[step, 0])
-        to_core(from_y, 0)
-        landed(from_y, 1, y_recv.at[step, 1])
-        to_x(from_y, 1, d_recv.at[step, 1])
-        to_core(from_y, 1)
-        landed(from_x, 1, x_recv.at[step, 1])
-        to_core(from_x, 1)
-    for step in range(outer):
-        block = block_of(step, d_spot)
-        for h in range(2):
-            landed(block, h, d_recv.at[step, h])
-            to_core(block, h)
-
-    seen = jnp.where(iota((SUB, LANES), 1) == me, 1.0, 0.0).astype(BF16)
-    codes = xb[:, :, 0:LANES].reshape(tokens, LANES)
-    code_row = lax.dot_general(
-        seen, codes, (((1,), (1,)), ((), ())), preferred_element_type=F32
-    )[0:1]
     groups = full + fold
-    packs = []
-    for g in range(groups):
-        r = iota((n * SUB, tokens), 0)
+
+    def experts(stage, join):
+        steps = stages[stage]
+        blocks = [pl.ds(block_of(step, 0), 4) for step in steps]
+        count = len(steps) * 4
+
+        def taken(ref, cols, size):
+            return jnp.concatenate(
+                [ref[block, :, cols].reshape(4 * rows, size) for block in blocks], axis=0
+            )
+
+        seen = jnp.where(iota((SUB, LANES), 1) == me, 1.0, 0.0).astype(BF16)
+        codes = taken(xb, pl.ds(0, LANES), LANES)
+        code_row = lax.dot_general(
+            seen, codes, (((1,), (1,)), ((), ())), preferred_element_type=F32
+        )[0:1]
+        shape = (count * SUB, count * rows)
+        r = iota(shape, 0)
         j = r % SUB
-        slot = g * SUB + (j if g < full else j % (SUB // 2))
-        same = (r // SUB) == (iota((n * SUB, tokens), 1) // rows)
-        hit = same & (code_row == (slot + 1).astype(F32))
-        packs.append(jnp.where(hit, 1.0, 0.0).astype(BF16))
-    pack = jnp.concatenate(packs, axis=0) if groups > 1 else packs[0]
-
-    for copy in w_loads[:4]:
-        copy.wait()
-    x_own = xb[:, :, LANES:].reshape(tokens, half)
-    gate = jnp.dot(x_own, wg[0], preferred_element_type=F32)
-    upper = jnp.dot(x_own, wu[0], preferred_element_type=F32)
-    remote(xp, xp, send_sem.at[0], recv_sem.at[0], tensor=other).wait_recv()
-    x_other = xp[...].reshape(tokens, half)
-    gate = gate + jnp.dot(x_other, wg[1], preferred_element_type=F32)
-    upper = upper + jnp.dot(x_other, wu[1], preferred_element_type=F32)
-    hidden = (gate / (1.0 + jnp.exp(-gate)) * upper).astype(BF16)
-    hid[core] = hidden
-    h_swap = remote(hid.at[core], hid.at[core], send_sem.at[6], recv_sem.at[3], tensor=other)
-    h_swap.start()
-
-    @pl.when(me < chunks)
-    def _():
+        same = (r // SUB) == (iota(shape, 1) // rows)
+        packs = []
+        for g in range(groups):
+            slot = g * SUB + (j if g < full else j % (SUB // 2))
+            hit = same & (code_row == (slot + 1).astype(F32))
+            packs.append(jnp.where(hit, 1.0, 0.0).astype(BF16))
+        pack = jnp.concatenate(packs, axis=0) if groups > 1 else packs[0]
+
+        if stage == 0:
+            for copy in w_loads[:4]:
+                copy.wait()
+        x_own = taken(xb, pl.ds(LANES, half), half)
+        gate = jnp.dot(x_own, wg[0], preferred_element_type=F32)
+        upper = jnp.dot(x_own, wu[0], preferred_element_type=F32)
+        arrived = xp.at[pl.ds(0, count)]
         remote(
-            apr.at[pl.ds(0, n - 1)],
-            apr.at[pl.ds(0, n - 1)],
-            send_sem.at[5],
-            recv_sem.at[2],
-            expert=x_side,
+            arrived, arrived, send_sem.at[0], recv_sem.at[7 + stage], tensor=other
         ).wait_recv()
-        apr[me] = aps[me]
-        peaks = apr[:, :, part_w : part_w + 1]
-        totals = apr[:, :, part_w + LANES // 2 : part_w + LANES // 2 + 1]
-        top = jnp.max(peaks, axis=0, keepdims=True)
-        scale = jnp.exp(peaks - top)
-        total = jnp.sum(totals * scale, axis=0)
-        joined = jnp.sum(apr[:, :, 0:part_w] * scale, axis=0)
-        ares[me] = (joined / total).astype(BF16)
-
-        def tell(step, carry):
+        x_other = taken(xp, pl.ds(0, half), half)
+        gate = gate + jnp.dot(x_other, wg[1], preferred_element_type=F32)
+        upper = upper + jnp.dot(x_other, wu[1], preferred_element_type=F32)
+        hidden = (gate / (1.0 + jnp.exp(-gate)) * upper).astype(BF16)
+        span = pl.ds(stage * early * 4 * rows, count * rows)
+        hid[core, span] = hidden
+        mine_hid = hid.at[core, span]
+        sems = ((6, 3), (10, 9))[stage]
+        swap = remote(mine_hid, mine_hid, send_sem.at[sems[0]], recv_sem.at[sems[1]], tensor=other)
+        swap.start()
+
+        if stage == 0:
+            w_loads[4].wait()
+            w_swap.wait_recv()
+        own_packed = jnp.dot(pack, hid[core, span], preferred_element_type=F32).astype(BF16)
+        value = jnp.dot(own_packed, wd[core], preferred_element_type=F32)
+        swap.wait_recv()
+        their_packed = jnp.dot(pack, hid[other, span], preferred_element_type=F32).astype(BF16)
+        value = (value + jnp.dot(their_packed, wd[other], preferred_element_type=F32)).astype(BF16)
+        left, right = value[:, :quarter], value[:, quarter:]
+        each = 4 * SUB
+        for g in range(groups):
+            for i, block in enumerate(blocks):
+                at = g * count * SUB + i * each
+                one, two = left[at : at + each], right[at : at + each]
+                if g < full:
+                    val[block, 2 * g] = one.reshape(4, SUB, quarter)
+                    val[block, 2 * g + 1] = two.reshape(4, SUB, quarter)
+                else:
+                    low = iota((each, quarter), 0) % SUB < SUB // 2
+                    val[block, 2 * full] = jnp.where(low, one, two).reshape(4, SUB, quarter)
+        join()
+        for step in reversed(steps):
+            for place in range(4):
+                dest = block_of(step, place)
+                copy = remote(
+                    val.at[dest], ret.at[me], send_sem.at[8], recv_sem.at[5], expert=dest
+                )
+                if step:
+                    copy.start()
+                else:
+                    pl.when(spot != place)(copy.start)
+        return swap
+
+    swap_early = experts(0, lambda: None)
+    across(1)
+
+    def join_attention():
+        @pl.when(me < chunks)
+        def _():
             remote(
-                ares.at[me],
-                ares.at[me],
-                send_sem.at[7],
-                recv_sem.at[4],
-                expert=lax.rem(me + step, n),
-            ).start()
-            return carry
-
-        lax.fori_loop(1, n, tell, 0)
-
-    w_loads[4].wait()
-    w_swap.wait_recv()
-    own_packed = jnp.dot(pack, hid[core], preferred_element_type=F32).astype(BF16)
-    value = jnp.dot(own_packed, wd[core], preferred_element_type=F32)
-    h_swap.wait_recv()
-    their_packed = jnp.dot(pack, hid[other], preferred_element_type=F32).astype(BF16)
-    value = (value + jnp.dot(their_packed, wd[other], preferred_element_type=F32)).astype(BF16)
-    left, right = value[:, :quarter], value[:, quarter:]
-    for g in range(full):
-        rs = slice(g * n * SUB, (g + 1) * n * SUB)
-        val[:, 2 * g] = left[rs].reshape(n, SUB, quarter)
-        val[:, 2 * g + 1] = right[rs].reshape(n, SUB, quarter)
-    if fold:
-        rs = slice(full * n * SUB, (full + 1) * n * SUB)
-        low = iota((n * SUB, quarter), 0) % SUB < SUB // 2
-        val[:, 2 * full] = jnp.where(low, left[rs], right[rs]).reshape(n, SUB, quarter)
-
-    def give(step, carry):
-        dest = lax.rem(me + step, n)
-        remote(val.at[dest], ret.at[me], send_sem.at[8], recv_sem.at[5], expert=dest).start()
-        return carry
-
-    lax.fori_loop(1, n, give, 0)
+                apr.at[pl.ds(0, n - 1)],
+                apr.at[pl.ds(0, n - 1)],
+                send_sem.at[5],
+                recv_sem.at[2],
+                expert=x_side,
+            ).wait_recv()
+            apr[me] = aps[me]
+            peaks = apr[:, :, part_w : part_w + 1]
+            totals = apr[:, :, part_w + LANES // 2 : part_w + LANES // 2 + 1]
+            top = jnp.max(peaks, axis=0, keepdims=True)
+            scale = jnp.exp(peaks - top)
+            total = jnp.sum(totals * scale, axis=0)
+            joined = jnp.sum(apr[:, :, 0:part_w] * scale, axis=0)
+            ares[me] = (joined / total).astype(BF16)
+
+            def tell(step, carry):
+                remote(
+                    ares.at[me],
+                    ares.at[me],
+                    send_sem.at[7],
+                    recv_sem.at[4],
+                    expert=lax.rem(me + step, n),
+                ).start()
+                return carry
+
+            lax.fori_loop(1, n, tell, 0)
+
+    swap_late = experts(1, join_attention)
     ret[me] = val[me]
 
-    high = gates // 16 * 16
-    spread_in = jnp.concatenate(
-        [high.astype(F32), (gates - high).astype(F32), code], axis=0
-    ).astype(BF16)
+    spread_in = jnp.concatenate([gate_high, gate_low, code], axis=0).astype(BF16)
     spot_of = jnp.where(
         iota((LANES, n * SUB), 0) == iota((LANES, n * SUB), 1) // SUB, 1.0, 0.0
     ).astype(BF16)
@@ -396,7 +447,8 @@
     part = xb.at[pl.ds(0, outer - 1)]
     remote(part, part, send_sem.at[3], recv_sem.at[0], expert=x_side).wait_send()
     w_swap.wait_send()
-    h_swap.wait_send()
+    swap_early.wait_send()
+    swap_late.wait_send()
 
     sent = chunks - jnp.where(me < chunks, 1, 0)
 
@@ -439,6 +491,24 @@
     remote(part, part, send_sem.at[8], recv_sem.at[5], expert=x_side).wait_send()
     o_swap.wait()
     moe_out[:, theirs] = op[...]
+
+
+def finish_kernel(moe, attn, moe_out, attn_out):
+    moe_out[...] = moe[...]
+    attn_out[...] = attn[...]
+
+
+def finish(moe, attn):
+    vmem = pl.BlockSpec(memory_space=pltpu.VMEM)
+    return pl.pallas_call(
+        finish_kernel,
+        out_shape=(
+            jax.ShapeDtypeStruct(moe.shape, BF16),
+            jax.ShapeDtypeStruct(attn.shape, BF16),
+        ),
+        in_specs=[vmem, vmem],
+        out_specs=(vmem, vmem),
+    )(moe, attn)
 
 
 def local(
@@ -473,7 +543,7 @@
     anywhere = pl.BlockSpec(memory_space=pl.ANY)
     vmem = pl.BlockSpec(memory_space=pltpu.VMEM)
     smem = pl.BlockSpec(memory_space=pltpu.SMEM)
-    return pl.pallas_call(
+    moe_out, attn_out = pl.pallas_call(
         functools.partial(kernel, n, full, fold, chunks),
         out_shape=(
             jax.ShapeDtypeStruct((rows, width), BF16),
@@ -515,8 +585,8 @@
             pltpu.SemaphoreType.DMA((outer, 2)),
             pltpu.SemaphoreType.DMA((outer, 2)),
             pltpu.SemaphoreType.DMA((outer, 2)),
+            pltpu.SemaphoreType.DMA((11,)),
             pltpu.SemaphoreType.DMA((10,)),
-            pltpu.SemaphoreType.DMA((7,)),
         ],
         compiler_params=pltpu.CompilerParams(
             collective_id=0, has_side_effects=True, vmem_limit_bytes=60 * 1024 * 1024
@@ -524,8 +594,8 @@
     )(
         hidden_in,
         batch_len,
-        expert_ids,
-        gate_num,
+        expert_ids.T,
+        gate_num.T,
         w_gate,
         w_up,
         w_down,
@@ -535,6 +605,7 @@
         kv_rope,
         ctx_len,
     )
+    return finish(moe_out, attn_out)
 
 
 def solution(mesh):

time: 55.3 us -> 45.4 us (0.82)
  local copies, waits for them, and re-layouts: 5.73 us -> 0 us
  Pallas kernels: 48 us -> 43.8 us
    pallas_call x1, Pallas kernels: 48 us -> 42.2 us  [local(): pl.pallas_call(functools.partial(kernel, n, full, fold, chunks), out_shap...]
    unnamed x4 -> x0, local copies, waits for them, and re-layouts: 5.73 us -> none
    pallas_call x0 -> x1, Pallas kernels: none -> 1.58 us  [finish(): pl.pallas_call(finish_kernel, out_shape=(jax.ShapeDtypeStruct(moe.shape,...]
where the time goes in v2:
time: 45.4 us; the launch traced here: 45 us
  Pallas kernels  43.8 us (96%)
  between operations  1.29 us (3%)
    pallas_call x1, Pallas kernels, local(): pl.pallas_call(functools.partial(kernel, n, full, fold, chunks), out_shap...  42.2 us
    pallas_call x1, Pallas kernels, finish(): pl.pallas_call(finish_kernel, out_shape=(jax.ShapeDtypeStruct(moe.shape,...  1.58 us

profile of v2, /device:TPU:15, one launch (start us, length us, event | category | flops | bytes accessed | tf_op | source)
XLA Modules:
  0.0 45.0 jit_solution(15501548655507247599)
XLA Ops:
  1.3 42.2 %shard_map.131 = (bf16[16,3584]{1,0:T(8,128)(2,1)}, bf16[2,32,512]{2,1,0:T(8,128)(2,1)}) custom-call(bf16[16,3584]{1,0:T(8,128)(2,1)} %x_hbm.1, s32[1]{0:T(128)S(6)} %copy.14.blen, s32[8,16]{1,0:T(8,128)} %bitcast.2, s32[8,16]{1,0:T(8,128)} %bitcast.3, bf16[1,3584,512]{2,1,0:T(8,128)(2,1)} %wg_hbm.1, bf16[1,3584,512]{2,1,0:T(8,128)(2,1)} %wu_hbm.1, ...), custom_call_target="tpu_custom_call" | custom-call | tf_op jit(solution)/shard_map/pallas_call | solution.py:546
  43.5 1.6 %shard_map.132 = (bf16[16,3584]{1,0:T(8,128)(2,1)}, bf16[2,32,512]{2,1,0:T(8,128)(2,1)}) custom-call(bf16[16,3584]{1,0:T(8,128)(2,1)} %get-tuple-element.4.moe, bf16[2,32,512]{2,1,0:T(8,128)(2,1)} %get-tuple-element.5.attn), custom_call_target="tpu_custom_call" | custom-call | tf_op jit(solution)/shard_map/pallas_call | solution.py:503
